TPU v7x, 256 devices: a whole 4x4x8 slice. The times are simulated.
256 devices in a mesh: tok: 32 (over z, y), head: 4 (over x), grp: 2 (over core).
Axes of the slice: x: 4, y: 4, z: 8, core: 2. Of those that a mesh axis runs over, the one named last changes fastest.
Arguments:
- tokens: bfloat16 [16384, 4096], P('tok', ('head', 'grp')), may hold values from -6 to 6
- norm_gain: bfloat16 [4096], P(('head', 'grp')), may hold values from 1.2 to 9, as said below
- query_key_value_weight: bfloat16 [4096, 6144], P(None, ('head', 'grp')), may hold values from -0.09375 to 0.09375
- out_weight: bfloat16 [4096, 4096], P(('head', 'grp')), may hold values from -0.09375 to 0.09375
- doc_ids: int32 [16384], P('tok'), may hold values from 0 to 15, never falling along the last dimension, each value on 1 to 8192 neighbouring positions
Outputs:
- attended: bfloat16 [16384, 4096], P('tok', ('head', 'grp'))
Inputs may be any that keep to these rules, and one draw needn't show every extreme that they name: `norm_gain`: norm gains are positive. `doc_ids`: non-decreasing along the window; each document has 1 to 8192 tokens and one has exactly 8192.
All inputs are finite; a program needn't handle non-finite values.
Results may differ from a plain program's by a relative error of at most 0.019.
The roundings to bfloat16 on the way count: a program that leaves them out, or rounds other values in their place, can miss the bound.
Values may be sent and summed in bfloat16 or wider, within the bound.
No kernel may reach another device: no remote copies, remote signals or barrier semaphores. Data moves between devices by JAX's collectives and lax.ppermute only.
A program may use at most 128 MiB of HBM per device.

v0:
```python
import jax
import jax.numpy as jnp
from jax import lax
from jax.sharding import PartitionSpec as P

QUERY_HEADS = 32
KEY_VALUE_HEADS = 8
HEAD_SIZE = 128
epsilon = 1e-05
theta = 500000.0
floor_score = -1e30


def rows_first(arrays, axis, dims):
    turned = [jnp.moveaxis(a, dim, 0) for a, dim in zip(arrays, dims)]
    both = jnp.concatenate([t.reshape(len(t), -1) for t in turned], axis=1)
    out, at, finished = (lax.all_gather(both, axis, axis=0, tiled=True), 0, [])
    for t, dim in zip(turned, dims):
        section = out[:, at : at + t[0].size].reshape(-1, *t.shape[1:])
        finished.append(jnp.moveaxis(section, 0, dim))
        at += t[0].size
    return tuple(finished)


def for_sending(array):

    def short(part):
        return part.astype(jnp.bfloat16) if part.dtype == jnp.float32 else part

    return jax.tree.map(short, array)


def passed_along(block, axis, distance):
    devices = range(lax.axis_size(axis))
    route = [((i - distance) % len(devices), i) for i in devices]
    return lax.ppermute(block, axis, route)


def rotate(vectors, positions):
    half = vectors.shape[-1] // 2
    inverse = 1.0 / theta ** (jnp.arange(half, dtype=jnp.float32) * (2.0 / vectors.shape[-1]))
    angles = positions.astype(jnp.float32)[:, None] * inverse[None, :]
    cosine = jnp.cos(angles)[:, None, :]
    sine = jnp.sin(angles)[:, None, :]
    first = vectors[..., :half]
    second = vectors[..., half:]
    return jnp.concatenate(
        [first * cosine - second * sine, second * cosine + first * sine], axis=-1
    )


def make_set(query_rows, positions, docs, head_group):
    length = query_rows.shape[0]
    flat = query_rows.reshape(length * head_group, query_rows.shape[1] // head_group)
    return (
        flat,
        jnp.repeat(positions, head_group),
        jnp.repeat(docs, head_group),
        docs[0],
        positions[length - 1],
    )


def empty_state(query_set):
    rows_all = query_set[0].shape[0]
    return (
        jnp.full((rows_all,), floor_score, jnp.float32),
        jnp.zeros((rows_all,), jnp.float32),
        jnp.zeros((rows_all, query_set[0].shape[1]), jnp.float32),
    )


def finish(state, head_group):
    highest, totals, accum = state
    normal = (accum / totals[:, None]).astype(jnp.bfloat16)
    return normal.reshape(normal.shape[0] // head_group, head_group * normal.shape[1])


def update(state, query_set, block_pairs, block_docs, block_positions):
    flat, query_positions, query_docs = (query_set[0], query_set[1], query_set[2])
    highest, totals, accum = state
    width = flat.shape[1]
    scores = lax.dot_general(
        flat, block_pairs[:, :width], (((1,), (1,)), ((), ())), preferred_element_type=jnp.float32
    ) * width ** (-0.5)
    mask = (block_positions[None, :] <= query_positions[:, None]) & (
        block_docs[None, :] == query_docs[:, None]
    )
    new_high = jnp.maximum(highest, jnp.max(jnp.where(mask, scores, floor_score), axis=1))
    weights = jnp.where(mask, jnp.exp(scores - new_high[:, None]), 0.0)
    fade = jnp.exp(highest - new_high)
    totals = totals * fade + jnp.sum(weights, axis=1)
    accum = accum * fade[:, None] + jnp.dot(
        weights.astype(jnp.bfloat16), block_pairs[:, width:], preferred_element_type=jnp.float32
    )
    return (new_high, totals, accum)


def fold_piece(state, query_set, pairs, docs, start):
    length = pairs.shape[0]
    width = 512

    def step(index, carried):
        offset = index * width
        first_key = start + offset
        block_positions = first_key + jnp.arange(width, dtype=jnp.int32)
        needed = (first_key <= query_set[4]) & (docs[width - 1] >= query_set[3])
        return lax.cond(
            needed,
            lambda held: update(held, query_set, pairs, docs, block_positions),
            lambda held: held,
            carried,
        )

    return lax.fori_loop(0, length // width, step, state)


def body(tokens, norm_gain, query_key_value_weight, out_weight, doc_ids):
    length = tokens.shape[0]
    head_group = QUERY_HEADS // KEY_VALUE_HEADS
    whole, gain = rows_first((tokens, norm_gain), ("head", "grp"), (1, 0))
    floats = whole.astype(jnp.float32)
    normed_input = (
        floats
        * lax.rsqrt(jnp.mean(floats * floats, axis=1, keepdims=True) + epsilon)
        * gain.astype(jnp.float32)
    ).astype(jnp.bfloat16)
    mixed_output = jnp.dot(normed_input, query_key_value_weight, preferred_element_type=jnp.float32)
    shard = lax.axis_index("tok")
    axis_size = lax.axis_size("tok")
    positions = shard * length + jnp.arange(length, dtype=jnp.int32)
    query_rows = (
        rotate(
            mixed_output[:, : head_group * HEAD_SIZE].reshape(length, head_group, HEAD_SIZE),
            positions,
        )
        .astype(jnp.bfloat16)
        .reshape(length, head_group * HEAD_SIZE)
    )
    keys = rotate(
        mixed_output[:, head_group * HEAD_SIZE : (head_group + 1) * HEAD_SIZE].reshape(
            length, 1, HEAD_SIZE
        ),
        positions,
    ).reshape(length, HEAD_SIZE)
    key_value = jnp.concatenate(
        [keys, mixed_output[:, (head_group + 1) * HEAD_SIZE :]], axis=1
    ).astype(jnp.bfloat16)
    query_sets = (make_set(query_rows, positions, doc_ids, head_group),)
    initial = tuple((empty_state(query_set) for query_set in query_sets))

    def fold_all(states, pieces, start):
        return tuple(
            (
                fold_piece(state, query_set, pieces[0], pieces[1], start)
                for state, query_set in zip(states, query_sets)
            )
        )

    reach = axis_size // 2
    first_states = fold_all(initial, (key_value, doc_ids), shard * length)

    def advance(step_index, carried):
        travelling, held = carried
        moved = jax.tree.map(
            lambda part, own: part.astype(own.dtype),
            passed_along(for_sending(travelling), "tok", 1),
            travelling,
        )
        anchor = jnp.mod(shard - step_index, axis_size)
        return (moved, fold_all(held, moved, anchor * length))

    states = lax.fori_loop(1, reach + 1, advance, ((key_value, doc_ids), first_states))[1]
    heads = finish(states[0], head_group)
    partial_products = jnp.dot(heads, out_weight, preferred_element_type=jnp.float32)
    return lax.psum_scatter(
        partial_products.astype(jnp.bfloat16), ("head", "grp"), scatter_dimension=1, tiled=True
    )


def solution(mesh):
    return jax.shard_map(
        body,
        mesh=mesh,
        in_specs=(
            P("tok", ("head", "grp")),
            P(("head", "grp")),
            P(None, ("head", "grp")),
            P(("head", "grp"), None),
            P("tok"),
        ),
        out_specs=P("tok", ("head", "grp")),
        check_vma=False,
    )
```

profile of v0, /device:TPU:8, one launch (start us, length us, event | category | flops | bytes accessed | tf_op | source)
XLA Modules:
  0.0 386.0 jit_solution(10557853256173840804)
XLA Ops:
  7.2 1.9 pad_maximum_fusion
  14.5 1.8 multiply_cosine_fusion
  16.3 30.7 %all-gather.2.cloned.1.call-done = bf16[4096,513]{0,1:T(8,128)(2,1)} async-done(((bf16[512,513]{0,1:T(8,128)(2,1)}), bf16[4096,513]{0,1:T(8,128)(2,1)}) %all-gather.2.cloned.1.call-update) | async-done | bytes 4202512 | tf_op jit(solution)/shard_map/all_gather | solution.py:17
  47.0 3.1 fusion.34
  51.0 7.2 %fusion.37 = f32[512,768]{1,0:T(8,128)S(1)} fusion(bf16[4096,768]{1,0:T(8,128)(2,1)} %param.13, f32[4096]{0:T(1024)S(1)} %bitcast.22, f32[512]{0:T(512)S(1)} %add_rsqrt_fusion, bf16[4096,513]{0,1:T(8,128)(2,1)} %all-gather.2.cloned.1.call-done), kind=kOutput, calls=%fused_computation.49 | convolution fusion | flops 3229614080 | bytes 12077056 | tf_op jit(solution)/shard_map/dot_general | solution.py:128
  62.8 1.8 subtract_convert_fusion
  64.9 5.6 %conditional.2 = ((f32[2048]{0:T(1024)S(1)}, f32[2048]{0:T(1024)S(1)}, f32[2048,128]{1,0:T(8,128)S(1)})) conditional(s32[]{:T(128)} %convert_element_type.61, (f32[2048]{0:T(1024)S(1)}, f32[2048]{0:T(1024)S(1)}, f32[2048,128]{1,0:T(8,128)S(1)}) %tuple.47, (s32[512]{0:T(512)S(1)}, s32[512]{0:T(512)S(1)}, s32[512]{0:T(512)S(1)}, s32[512]{0:T(512)S(1)}, ...), branch_computations={%region_1.2_spmd, %region_2.5_spmd} | conditional | flops 558370816 | bytes 16236576 | solution.py:108
  68.4 1.8 convolution_add_fusion
  70.5 199.8 %while.46 = (s32[]{:T(128)}, bf16[512,256]{1,0:T(8,128)(2,1)S(1)}, s32[512]{0:T(512)S(1)}, f32[2048]{0:T(1024)S(1)}, f32[2048]{0:T(1024)S(1)}, /*index=5*/f32[20...) while((s32[]{:T(128)}, bf16[512,256]{1,0:T(8,128)(2,1)S(1)}, ...), condition=%wide.region_10.11_spmd.clone, body=%wide.region_5.10_spmd.clone.sunk | while | flops 558371328 | bytes 17304096 | solution.py:173
  74.0 5.1 %collective-permute-done.1 = s32[512]{0:T(512)S(1)} collective-permute-done((s32[512]{0:T(512)S(1)}, s32[512]{0:T(512)S(1)}, u32[]{:S(2)}, u32[]{:S(2)}) %collective-permute-start.1) | collective-permute-done | bytes 2080 | tf_op jit(solution)/shard_map/while/body/eval_jaxpr/ppermute | solution.py:36
  80.9 5.3 %conditional.5 = ((f32[2048]{0:T(1024)S(1)}, f32[2048]{0:T(1024)S(1)}, f32[2048,128]{1,0:T(8,128)S(1)})) conditional(s32[]{:T(128)} %convert_element_type.86, (f32[2048]{0:T(1024)S(1)}, f32[2048]{0:T(1024)S(1)}, f32[2048,128]{1,0:T(8,128)S(1)}) %tuple.76, (s32[]{:T(128)}, s32[512]{0:T(512)S(1)}, s32[512]{0:T(512)S(1)}, s32[512]{0:T(512)S(1)}, ...), branch_computations={%region_6.6_spmd, %region_7.9_spmd} | conditional | flops 558371328 | bytes 15716388 | solution.py:108
  82.6 1.6 fusion.20
  84.3 1.8 convolution_add_fusion.1
  89.6 4.3 %collective-permute-done.1 = s32[512]{0:T(512)S(1)} collective-permute-done((s32[512]{0:T(512)S(1)}, s32[512]{0:T(512)S(1)}, u32[]{:S(2)}, u32[]{:S(2)}) %collective-permute-start.1) | collective-permute-done | bytes 2080 | tf_op jit(solution)/shard_map/while/body/eval_jaxpr/ppermute | solution.py:36
  95.7 6.8 %collective-permute-start = (bf16[512,256]{1,0:T(8,128)(2,1)S(1)}, bf16[512,256]{1,0:T(8,128)(2,1)S(1)}, u32[]{:S(2)}, u32[]{:S(2)}) collective-permute-start(bf16[512,256]{1,0:T(8,128)(2,1)S(1)} %get-tuple-element.702), channel_id=1, source_target_pairs={{248,0},{0,8},{8,16},{16,24},{24,32},{32,40},{40,48},{48,56},{56,6... | collective-permute-start | bytes 786440 | tf_op jit(solution)/shard_map/while/body/eval_jaxpr/ppermute | solution.py:36
  103.3 3.5 collective-permute-done.1
  108.7 2.6 collective-permute-start
  112.2 4.7 %collective-permute-done.1 = s32[512]{0:T(512)S(1)} collective-permute-done((s32[512]{0:T(512)S(1)}, s32[512]{0:T(512)S(1)}, u32[]{:S(2)}, u32[]{:S(2)}) %collective-permute-start.1) | collective-permute-done | bytes 2080 | tf_op jit(solution)/shard_map/while/body/eval_jaxpr/ppermute | solution.py:36
  121.7 6.7 %collective-permute-done.1 = s32[512]{0:T(512)S(1)} collective-permute-done((s32[512]{0:T(512)S(1)}, s32[512]{0:T(512)S(1)}, u32[]{:S(2)}, u32[]{:S(2)}) %collective-permute-start.1) | collective-permute-done | bytes 2080 | tf_op jit(solution)/shard_map/while/body/eval_jaxpr/ppermute | solution.py:36
  130.3 2.6 collective-permute-start.1
  133.6 6.4 %collective-permute-done.1 = s32[512]{0:T(512)S(1)} collective-permute-done((s32[512]{0:T(512)S(1)}, s32[512]{0:T(512)S(1)}, u32[]{:S(2)}, u32[]{:S(2)}) %collective-permute-start.1) | collective-permute-done | bytes 2080 | tf_op jit(solution)/shard_map/while/body/eval_jaxpr/ppermute | solution.py:36
  141.9 6.7 %collective-permute-start.1 = (s32[512]{0:T(512)S(1)}, s32[512]{0:T(512)S(1)}, u32[]{:S(2)}, u32[]{:S(2)}) collective-permute-start(s32[512]{0:T(512)S(1)} %get-tuple-element.703), channel_id=1, source_target_pairs={{248,0},{0,8},{8,16},{16,24},{24,32},{32,40},{40,48},{48,56},{56,6... | collective-permute-start | bytes 6152 | tf_op jit(solution)/shard_map/while/body/eval_jaxpr/ppermute | solution.py:36
  149.3 2.3 collective-permute-done.1
  153.5 3.0 collective-permute-start
  156.4 2.6 collective-permute-start.1
  159.7 3.5 collective-permute-done.1
  165.1 7.0 %collective-permute-start = (bf16[512,256]{1,0:T(8,128)(2,1)S(1)}, bf16[512,256]{1,0:T(8,128)(2,1)S(1)}, u32[]{:S(2)}, u32[]{:S(2)}) collective-permute-start(bf16[512,256]{1,0:T(8,128)(2,1)S(1)} %get-tuple-element.702), channel_id=1, source_target_pairs={{248,0},{0,8},{8,16},{16,24},{24,32},{32,40},{40,48},{48,56},{56,6... | collective-permute-start | bytes 786440 | tf_op jit(solution)/shard_map/while/body/eval_jaxpr/ppermute | solution.py:36
  172.1 4.1 %collective-permute-start.1 = (s32[512]{0:T(512)S(1)}, s32[512]{0:T(512)S(1)}, u32[]{:S(2)}, u32[]{:S(2)}) collective-permute-start(s32[512]{0:T(512)S(1)} %get-tuple-element.703), channel_id=1, source_target_pairs={{248,0},{0,8},{8,16},{16,24},{24,32},{32,40},{40,48},{48,56},{56,6... | collective-permute-start | bytes 6152 | tf_op jit(solution)/shard_map/while/body/eval_jaxpr/ppermute | solution.py:36
  176.8 1.7 collective-permute-done.1
  180.4 3.8 collective-permute-start
  184.2 4.9 %collective-permute-start.1 = (s32[512]{0:T(512)S(1)}, s32[512]{0:T(512)S(1)}, u32[]{:S(2)}, u32[]{:S(2)}) collective-permute-start(s32[512]{0:T(512)S(1)} %get-tuple-element.703), channel_id=1, source_target_pairs={{248,0},{0,8},{8,16},{16,24},{24,32},{32,40},{40,48},{48,56},{56,6... | collective-permute-start | bytes 6152 | tf_op jit(solution)/shard_map/while/body/eval_jaxpr/ppermute | solution.py:36
  192.5 4.7 %collective-permute-start = (bf16[512,256]{1,0:T(8,128)(2,1)S(1)}, bf16[512,256]{1,0:T(8,128)(2,1)S(1)}, u32[]{:S(2)}, u32[]{:S(2)}) collective-permute-start(bf16[512,256]{1,0:T(8,128)(2,1)S(1)} %get-tuple-element.702), channel_id=1, source_target_pairs={{248,0},{0,8},{8,16},{16,24},{24,32},{32,40},{40,48},{48,56},{56,6... | collective-permute-start | bytes 786440 | tf_op jit(solution)/shard_map/while/body/eval_jaxpr/ppermute | solution.py:36
  197.2 4.4 %collective-permute-start.1 = (s32[512]{0:T(512)S(1)}, s32[512]{0:T(512)S(1)}, u32[]{:S(2)}, u32[]{:S(2)}) collective-permute-start(s32[512]{0:T(512)S(1)} %get-tuple-element.703), channel_id=1, source_target_pairs={{248,0},{0,8},{8,16},{16,24},{24,32},{32,40},{40,48},{48,56},{56,6... | collective-permute-start | bytes 6152 | tf_op jit(solution)/shard_map/while/body/eval_jaxpr/ppermute | solution.py:36
  202.2 1.8 collective-permute-done.1
  205.9 3.5 collective-permute-start
  209.3 3.7 collective-permute-start.1
  213.7 3.3 collective-permute-done.1
  218.9 2.0 collective-permute-start
  220.9 2.9 collective-permute-start.1
  224.4 4.8 %collective-permute-done.1 = s32[512]{0:T(512)S(1)} collective-permute-done((s32[512]{0:T(512)S(1)}, s32[512]{0:T(512)S(1)}, u32[]{:S(2)}, u32[]{:S(2)}) %collective-permute-start.1) | collective-permute-done | bytes 2080 | tf_op jit(solution)/shard_map/while/body/eval_jaxpr/ppermute | solution.py:36
  231.5 3.9 %collective-permute-start.1 = (s32[512]{0:T(512)S(1)}, s32[512]{0:T(512)S(1)}, u32[]{:S(2)}, u32[]{:S(2)}) collective-permute-start(s32[512]{0:T(512)S(1)} %get-tuple-element.703), channel_id=1, source_target_pairs={{248,0},{0,8},{8,16},{16,24},{24,32},{32,40},{40,48},{48,56},{56,6... | collective-permute-start | bytes 6152 | tf_op jit(solution)/shard_map/while/body/eval_jaxpr/ppermute | solution.py:36
  236.2 4.4 %collective-permute-done.1 = s32[512]{0:T(512)S(1)} collective-permute-done((s32[512]{0:T(512)S(1)}, s32[512]{0:T(512)S(1)}, u32[]{:S(2)}, u32[]{:S(2)}) %collective-permute-start.1) | collective-permute-done | bytes 2080 | tf_op jit(solution)/shard_map/while/body/eval_jaxpr/ppermute | solution.py:36
  242.4 5.4 %collective-permute-start = (bf16[512,256]{1,0:T(8,128)(2,1)S(1)}, bf16[512,256]{1,0:T(8,128)(2,1)S(1)}, u32[]{:S(2)}, u32[]{:S(2)}) collective-permute-start(bf16[512,256]{1,0:T(8,128)(2,1)S(1)} %get-tuple-element.702), channel_id=1, source_target_pairs={{248,0},{0,8},{8,16},{16,24},{24,32},{32,40},{40,48},{48,56},{56,6... | collective-permute-start | bytes 786440 | tf_op jit(solution)/shard_map/while/body/eval_jaxpr/ppermute | solution.py:36
  247.7 5.1 %collective-permute-start.1 = (s32[512]{0:T(512)S(1)}, s32[512]{0:T(512)S(1)}, u32[]{:S(2)}, u32[]{:S(2)}) collective-permute-start(s32[512]{0:T(512)S(1)} %get-tuple-element.703), channel_id=1, source_target_pairs={{248,0},{0,8},{8,16},{16,24},{24,32},{32,40},{40,48},{48,56},{56,6... | collective-permute-start | bytes 6152 | tf_op jit(solution)/shard_map/while/body/eval_jaxpr/ppermute | solution.py:36
  256.0 5.5 %collective-permute-start = (bf16[512,256]{1,0:T(8,128)(2,1)S(1)}, bf16[512,256]{1,0:T(8,128)(2,1)S(1)}, u32[]{:S(2)}, u32[]{:S(2)}) collective-permute-start(bf16[512,256]{1,0:T(8,128)(2,1)S(1)} %get-tuple-element.702), channel_id=1, source_target_pairs={{248,0},{0,8},{8,16},{16,24},{24,32},{32,40},{40,48},{48,56},{56,6... | collective-permute-start | bytes 786440 | tf_op jit(solution)/shard_map/while/body/eval_jaxpr/ppermute | solution.py:36
  261.5 5.7 %collective-permute-start.1 = (s32[512]{0:T(512)S(1)}, s32[512]{0:T(512)S(1)}, u32[]{:S(2)}, u32[]{:S(2)}) collective-permute-start(s32[512]{0:T(512)S(1)} %get-tuple-element.703), channel_id=1, source_target_pairs={{248,0},{0,8},{8,16},{16,24},{24,32},{32,40},{40,48},{48,56},{56,6... | collective-permute-start | bytes 6152 | tf_op jit(solution)/shard_map/while/body/eval_jaxpr/ppermute | solution.py:36
  271.0 6.5 %convolution_convert_fusion = bf16[512,4096]{1,0:T(8,128)(2,1)} fusion(bf16[512,512]{1,0:T(8,128)(2,1)S(1)} %reshape.157, bf16[512,4096]{1,0:T(8,128)(2,1)} %param.14), kind=kOutput, calls=%fused_computation.48 | convolution fusion | flops 2149580800 | bytes 8912896 | tf_op jit(solution)/shard_map/dot_general | solution.py:175
  277.5 101.6 %reduce-scatter.2.cloned.1.call-done = bf16[512,512]{1,0:T(8,128)(2,1)} async-done(((bf16[512,4096]{1,0:T(8,128)(2,1)}), bf16[512,512]{1,0:T(8,128)(2,1)}) %reduce-scatter.2.cloned.1.call-update) | async-done | bytes 524304 | tf_op jit(solution)/shard_map/reduce_scatter | solution.py:176
  (170 shorter events, 36.7 us)
Async XLA Ops:
  6.5 40.5 %all-gather.2.cloned.1.call-start = ((), (), s32[]{:S(2)}) async-start(), calls=%async_computation.1 | async-start | bytes 4792320 | tf_op jit(solution)/shard_map/all_gather | solution.py:17
  9.1 370.0 %reduce-scatter.2.cloned.1.call-start = ((), (), s32[]{:S(2)}) async-start(), calls=%async_computation.2 | async-start | bytes 4718592 | tf_op jit(solution)/shard_map/reduce_scatter | solution.py:176
  9.2 5.2 %copy-start.2 = (s32[512]{0:T(512)}, s32[512]{0:T(512)S(1)}, u32[]{:S(2)}) copy-start(s32[512]{0:T(512)S(1)} %get-tuple-element.694) | copy-start | bytes 6148
  9.2 49.0 %copy-start.4 = (f32[512]{0:T(512)}, f32[512]{0:T(512)S(1)}, u32[]{:S(2)}) copy-start(f32[512]{0:T(512)S(1)} %get-tuple-element.592) | copy-start | bytes 6148
  14.5 1.8 copy-start.5
  61.9 3.0 copy-start.1
  61.9 3.0 copy-start.3
  64.9 5.6 %copy-start = (bf16[512,256]{1,0:T(8,128)(2,1)S(1)}, bf16[512,256]{1,0:T(8,128)(2,1)}, u32[]{:S(2)}) copy-start(bf16[512,256]{1,0:T(8,128)(2,1)} %copy.9) | copy-start | bytes 786436
  64.9 5.6 %copy-start.6 = (s32[512]{0:T(512)S(1)}, s32[512]{0:T(512)}, u32[]{:S(2)}) copy-start(s32[512]{0:T(512)} %copy.26) | copy-start | bytes 6148
  70.5 10.3 %collective-permute-start = (bf16[512,256]{1,0:T(8,128)(2,1)S(1)}, bf16[512,256]{1,0:T(8,128)(2,1)S(1)}, u32[]{:S(2)}, u32[]{:S(2)}) collective-permute-start(bf16[512,256]{1,0:T(8,128)(2,1)S(1)} %get-tuple-element.702), channel_id=1, source_target_pairs={{248,0},{0,8},{8,16},{16,24},{24,32},{32,40},{40,48},{48,56},{56,6... | collective-permute-start | bytes 786440 | tf_op jit(solution)/shard_map/while/body/eval_jaxpr/ppermute | solution.py:36
  72.1 7.0 %collective-permute-start.1 = (s32[512]{0:T(512)S(1)}, s32[512]{0:T(512)S(1)}, u32[]{:S(2)}, u32[]{:S(2)}) collective-permute-start(s32[512]{0:T(512)S(1)} %get-tuple-element.703), channel_id=1, source_target_pairs={{248,0},{0,8},{8,16},{16,24},{24,32},{32,40},{40,48},{48,56},{56,6... | collective-permute-start | bytes 6152 | tf_op jit(solution)/shard_map/while/body/eval_jaxpr/ppermute | solution.py:36
  86.2 9.5 %collective-permute-start = (bf16[512,256]{1,0:T(8,128)(2,1)S(1)}, bf16[512,256]{1,0:T(8,128)(2,1)S(1)}, u32[]{:S(2)}, u32[]{:S(2)}) collective-permute-start(bf16[512,256]{1,0:T(8,128)(2,1)S(1)} %get-tuple-element.702), channel_id=1, source_target_pairs={{248,0},{0,8},{8,16},{16,24},{24,32},{32,40},{40,48},{48,56},{56,6... | collective-permute-start | bytes 786440 | tf_op jit(solution)/shard_map/while/body/eval_jaxpr/ppermute | solution.py:36
  87.7 6.2 %collective-permute-start.1 = (s32[512]{0:T(512)S(1)}, s32[512]{0:T(512)S(1)}, u32[]{:S(2)}, u32[]{:S(2)}) collective-permute-start(s32[512]{0:T(512)S(1)} %get-tuple-element.703), channel_id=1, source_target_pairs={{248,0},{0,8},{8,16},{16,24},{24,32},{32,40},{40,48},{48,56},{56,6... | collective-permute-start | bytes 6152 | tf_op jit(solution)/shard_map/while/body/eval_jaxpr/ppermute | solution.py:36
  95.7 12.9 %collective-permute-start = (bf16[512,256]{1,0:T(8,128)(2,1)S(1)}, bf16[512,256]{1,0:T(8,128)(2,1)S(1)}, u32[]{:S(2)}, u32[]{:S(2)}) collective-permute-start(bf16[512,256]{1,0:T(8,128)(2,1)S(1)} %get-tuple-element.702), channel_id=1, source_target_pairs={{248,0},{0,8},{8,16},{16,24},{24,32},{32,40},{40,48},{48,56},{56,6... | collective-permute-start | bytes 786440 | tf_op jit(solution)/shard_map/while/body/eval_jaxpr/ppermute | solution.py:36
  102.5 4.3 %collective-permute-start.1 = (s32[512]{0:T(512)S(1)}, s32[512]{0:T(512)S(1)}, u32[]{:S(2)}, u32[]{:S(2)}) collective-permute-start(s32[512]{0:T(512)S(1)} %get-tuple-element.703), channel_id=1, source_target_pairs={{248,0},{0,8},{8,16},{16,24},{24,32},{32,40},{40,48},{48,56},{56,6... | collective-permute-start | bytes 6152 | tf_op jit(solution)/shard_map/while/body/eval_jaxpr/ppermute | solution.py:36
  108.7 9.9 %collective-permute-start = (bf16[512,256]{1,0:T(8,128)(2,1)S(1)}, bf16[512,256]{1,0:T(8,128)(2,1)S(1)}, u32[]{:S(2)}, u32[]{:S(2)}) collective-permute-start(bf16[512,256]{1,0:T(8,128)(2,1)S(1)} %get-tuple-element.702), channel_id=1, source_target_pairs={{248,0},{0,8},{8,16},{16,24},{24,32},{32,40},{40,48},{48,56},{56,6... | collective-permute-start | bytes 786440 | tf_op jit(solution)/shard_map/while/body/eval_jaxpr/ppermute | solution.py:36
  111.2 5.6 %collective-permute-start.1 = (s32[512]{0:T(512)S(1)}, s32[512]{0:T(512)S(1)}, u32[]{:S(2)}, u32[]{:S(2)}) collective-permute-start(s32[512]{0:T(512)S(1)} %get-tuple-element.703), channel_id=1, source_target_pairs={{248,0},{0,8},{8,16},{16,24},{24,32},{32,40},{40,48},{48,56},{56,6... | collective-permute-start | bytes 6152 | tf_op jit(solution)/shard_map/while/body/eval_jaxpr/ppermute | solution.py:36
  118.7 11.4 %collective-permute-start = (bf16[512,256]{1,0:T(8,128)(2,1)S(1)}, bf16[512,256]{1,0:T(8,128)(2,1)S(1)}, u32[]{:S(2)}, u32[]{:S(2)}) collective-permute-start(bf16[512,256]{1,0:T(8,128)(2,1)S(1)} %get-tuple-element.702), channel_id=1, source_target_pairs={{248,0},{0,8},{8,16},{16,24},{24,32},{32,40},{40,48},{48,56},{56,6... | collective-permute-start | bytes 786440 | tf_op jit(solution)/shard_map/while/body/eval_jaxpr/ppermute | solution.py:36
  119.5 8.9 %collective-permute-start.1 = (s32[512]{0:T(512)S(1)}, s32[512]{0:T(512)S(1)}, u32[]{:S(2)}, u32[]{:S(2)}) collective-permute-start(s32[512]{0:T(512)S(1)} %get-tuple-element.703), channel_id=1, source_target_pairs={{248,0},{0,8},{8,16},{16,24},{24,32},{32,40},{40,48},{48,56},{56,6... | collective-permute-start | bytes 6152 | tf_op jit(solution)/shard_map/while/body/eval_jaxpr/ppermute | solution.py:36
  130.2 11.5 %collective-permute-start = (bf16[512,256]{1,0:T(8,128)(2,1)S(1)}, bf16[512,256]{1,0:T(8,128)(2,1)S(1)}, u32[]{:S(2)}, u32[]{:S(2)}) collective-permute-start(bf16[512,256]{1,0:T(8,128)(2,1)S(1)} %get-tuple-element.702), channel_id=1, source_target_pairs={{248,0},{0,8},{8,16},{16,24},{24,32},{32,40},{40,48},{48,56},{56,6... | collective-permute-start | bytes 786440 | tf_op jit(solution)/shard_map/while/body/eval_jaxpr/ppermute | solution.py:36
  130.3 9.7 %collective-permute-start.1 = (s32[512]{0:T(512)S(1)}, s32[512]{0:T(512)S(1)}, u32[]{:S(2)}, u32[]{:S(2)}) collective-permute-start(s32[512]{0:T(512)S(1)} %get-tuple-element.703), channel_id=1, source_target_pairs={{248,0},{0,8},{8,16},{16,24},{24,32},{32,40},{40,48},{48,56},{56,6... | collective-permute-start | bytes 6152 | tf_op jit(solution)/shard_map/while/body/eval_jaxpr/ppermute | solution.py:36
  141.8 11.5 %collective-permute-start = (bf16[512,256]{1,0:T(8,128)(2,1)S(1)}, bf16[512,256]{1,0:T(8,128)(2,1)S(1)}, u32[]{:S(2)}, u32[]{:S(2)}) collective-permute-start(bf16[512,256]{1,0:T(8,128)(2,1)S(1)} %get-tuple-element.702), channel_id=1, source_target_pairs={{248,0},{0,8},{8,16},{16,24},{24,32},{32,40},{40,48},{48,56},{56,6... | collective-permute-start | bytes 786440 | tf_op jit(solution)/shard_map/while/body/eval_jaxpr/ppermute | solution.py:36
  141.9 9.7 %collective-permute-start.1 = (s32[512]{0:T(512)S(1)}, s32[512]{0:T(512)S(1)}, u32[]{:S(2)}, u32[]{:S(2)}) collective-permute-start(s32[512]{0:T(512)S(1)} %get-tuple-element.703), channel_id=1, source_target_pairs={{248,0},{0,8},{8,16},{16,24},{24,32},{32,40},{40,48},{48,56},{56,6... | collective-permute-start | bytes 6152 | tf_op jit(solution)/shard_map/while/body/eval_jaxpr/ppermute | solution.py:36
  153.5 11.5 %collective-permute-start = (bf16[512,256]{1,0:T(8,128)(2,1)S(1)}, bf16[512,256]{1,0:T(8,128)(2,1)S(1)}, u32[]{:S(2)}, u32[]{:S(2)}) collective-permute-start(bf16[512,256]{1,0:T(8,128)(2,1)S(1)} %get-tuple-element.702), channel_id=1, source_target_pairs={{248,0},{0,8},{8,16},{16,24},{24,32},{32,40},{40,48},{48,56},{56,6... | collective-permute-start | bytes 786440 | tf_op jit(solution)/shard_map/while/body/eval_jaxpr/ppermute | solution.py:36
  156.4 6.8 %collective-permute-start.1 = (s32[512]{0:T(512)S(1)}, s32[512]{0:T(512)S(1)}, u32[]{:S(2)}, u32[]{:S(2)}) collective-permute-start(s32[512]{0:T(512)S(1)} %get-tuple-element.703), channel_id=1, source_target_pairs={{248,0},{0,8},{8,16},{16,24},{24,32},{32,40},{40,48},{48,56},{56,6... | collective-permute-start | bytes 6152 | tf_op jit(solution)/shard_map/while/body/eval_jaxpr/ppermute | solution.py:36
  165.1 15.2 %collective-permute-start = (bf16[512,256]{1,0:T(8,128)(2,1)S(1)}, bf16[512,256]{1,0:T(8,128)(2,1)S(1)}, u32[]{:S(2)}, u32[]{:S(2)}) collective-permute-start(bf16[512,256]{1,0:T(8,128)(2,1)S(1)} %get-tuple-element.702), channel_id=1, source_target_pairs={{248,0},{0,8},{8,16},{16,24},{24,32},{32,40},{40,48},{48,56},{56,6... | collective-permute-start | bytes 786440 | tf_op jit(solution)/shard_map/while/body/eval_jaxpr/ppermute | solution.py:36
  172.1 6.5 %collective-permute-start.1 = (s32[512]{0:T(512)S(1)}, s32[512]{0:T(512)S(1)}, u32[]{:S(2)}, u32[]{:S(2)}) collective-permute-start(s32[512]{0:T(512)S(1)} %get-tuple-element.703), channel_id=1, source_target_pairs={{248,0},{0,8},{8,16},{16,24},{24,32},{32,40},{40,48},{48,56},{56,6... | collective-permute-start | bytes 6152 | tf_op jit(solution)/shard_map/while/body/eval_jaxpr/ppermute | solution.py:36
  180.4 12.0 %collective-permute-start = (bf16[512,256]{1,0:T(8,128)(2,1)S(1)}, bf16[512,256]{1,0:T(8,128)(2,1)S(1)}, u32[]{:S(2)}, u32[]{:S(2)}) collective-permute-start(bf16[512,256]{1,0:T(8,128)(2,1)S(1)} %get-tuple-element.702), channel_id=1, source_target_pairs={{248,0},{0,8},{8,16},{16,24},{24,32},{32,40},{40,48},{48,56},{56,6... | collective-permute-start | bytes 786440 | tf_op jit(solution)/shard_map/while/body/eval_jaxpr/ppermute | solution.py:36
  184.2 6.4 %collective-permute-start.1 = (s32[512]{0:T(512)S(1)}, s32[512]{0:T(512)S(1)}, u32[]{:S(2)}, u32[]{:S(2)}) collective-permute-start(s32[512]{0:T(512)S(1)} %get-tuple-element.703), channel_id=1, source_target_pairs={{248,0},{0,8},{8,16},{16,24},{24,32},{32,40},{40,48},{48,56},{56,6... | collective-permute-start | bytes 6152 | tf_op jit(solution)/shard_map/while/body/eval_jaxpr/ppermute | solution.py:36
  192.5 13.3 %collective-permute-start = (bf16[512,256]{1,0:T(8,128)(2,1)S(1)}, bf16[512,256]{1,0:T(8,128)(2,1)S(1)}, u32[]{:S(2)}, u32[]{:S(2)}) collective-permute-start(bf16[512,256]{1,0:T(8,128)(2,1)S(1)} %get-tuple-element.702), channel_id=1, source_target_pairs={{248,0},{0,8},{8,16},{16,24},{24,32},{32,40},{40,48},{48,56},{56,6... | collective-permute-start | bytes 786440 | tf_op jit(solution)/shard_map/while/body/eval_jaxpr/ppermute | solution.py:36
  197.2 6.9 %collective-permute-start.1 = (s32[512]{0:T(512)S(1)}, s32[512]{0:T(512)S(1)}, u32[]{:S(2)}, u32[]{:S(2)}) collective-permute-start(s32[512]{0:T(512)S(1)} %get-tuple-element.703), channel_id=1, source_target_pairs={{248,0},{0,8},{8,16},{16,24},{24,32},{32,40},{40,48},{48,56},{56,6... | collective-permute-start | bytes 6152 | tf_op jit(solution)/shard_map/while/body/eval_jaxpr/ppermute | solution.py:36
  205.9 12.9 %collective-permute-start = (bf16[512,256]{1,0:T(8,128)(2,1)S(1)}, bf16[512,256]{1,0:T(8,128)(2,1)S(1)}, u32[]{:S(2)}, u32[]{:S(2)}) collective-permute-start(bf16[512,256]{1,0:T(8,128)(2,1)S(1)} %get-tuple-element.702), channel_id=1, source_target_pairs={{248,0},{0,8},{8,16},{16,24},{24,32},{32,40},{40,48},{48,56},{56,6... | collective-permute-start | bytes 786440 | tf_op jit(solution)/shard_map/while/body/eval_jaxpr/ppermute | solution.py:36
  209.3 7.7 %collective-permute-start.1 = (s32[512]{0:T(512)S(1)}, s32[512]{0:T(512)S(1)}, u32[]{:S(2)}, u32[]{:S(2)}) collective-permute-start(s32[512]{0:T(512)S(1)} %get-tuple-element.703), channel_id=1, source_target_pairs={{248,0},{0,8},{8,16},{16,24},{24,32},{32,40},{40,48},{48,56},{56,6... | collective-permute-start | bytes 6152 | tf_op jit(solution)/shard_map/while/body/eval_jaxpr/ppermute | solution.py:36
  218.9 12.1 %collective-permute-start = (bf16[512,256]{1,0:T(8,128)(2,1)S(1)}, bf16[512,256]{1,0:T(8,128)(2,1)S(1)}, u32[]{:S(2)}, u32[]{:S(2)}) collective-permute-start(bf16[512,256]{1,0:T(8,128)(2,1)S(1)} %get-tuple-element.702), channel_id=1, source_target_pairs={{248,0},{0,8},{8,16},{16,24},{24,32},{32,40},{40,48},{48,56},{56,6... | collective-permute-start | bytes 786440 | tf_op jit(solution)/shard_map/while/body/eval_jaxpr/ppermute | solution.py:36
  220.9 8.4 %collective-permute-start.1 = (s32[512]{0:T(512)S(1)}, s32[512]{0:T(512)S(1)}, u32[]{:S(2)}, u32[]{:S(2)}) collective-permute-start(s32[512]{0:T(512)S(1)} %get-tuple-element.703), channel_id=1, source_target_pairs={{248,0},{0,8},{8,16},{16,24},{24,32},{32,40},{40,48},{48,56},{56,6... | collective-permute-start | bytes 6152 | tf_op jit(solution)/shard_map/while/body/eval_jaxpr/ppermute | solution.py:36
  231.0 11.3 %collective-permute-start = (bf16[512,256]{1,0:T(8,128)(2,1)S(1)}, bf16[512,256]{1,0:T(8,128)(2,1)S(1)}, u32[]{:S(2)}, u32[]{:S(2)}) collective-permute-start(bf16[512,256]{1,0:T(8,128)(2,1)S(1)} %get-tuple-element.702), channel_id=1, source_target_pairs={{248,0},{0,8},{8,16},{16,24},{24,32},{32,40},{40,48},{48,56},{56,6... | collective-permute-start | bytes 786440 | tf_op jit(solution)/shard_map/while/body/eval_jaxpr/ppermute | solution.py:36
  231.5 9.0 %collective-permute-start.1 = (s32[512]{0:T(512)S(1)}, s32[512]{0:T(512)S(1)}, u32[]{:S(2)}, u32[]{:S(2)}) collective-permute-start(s32[512]{0:T(512)S(1)} %get-tuple-element.703), channel_id=1, source_target_pairs={{248,0},{0,8},{8,16},{16,24},{24,32},{32,40},{40,48},{48,56},{56,6... | collective-permute-start | bytes 6152 | tf_op jit(solution)/shard_map/while/body/eval_jaxpr/ppermute | solution.py:36
  242.4 13.5 %collective-permute-start = (bf16[512,256]{1,0:T(8,128)(2,1)S(1)}, bf16[512,256]{1,0:T(8,128)(2,1)S(1)}, u32[]{:S(2)}, u32[]{:S(2)}) collective-permute-start(bf16[512,256]{1,0:T(8,128)(2,1)S(1)} %get-tuple-element.702), channel_id=1, source_target_pairs={{248,0},{0,8},{8,16},{16,24},{24,32},{32,40},{40,48},{48,56},{56,6... | collective-permute-start | bytes 786440 | tf_op jit(solution)/shard_map/while/body/eval_jaxpr/ppermute | solution.py:36
  247.7 6.4 %collective-permute-start.1 = (s32[512]{0:T(512)S(1)}, s32[512]{0:T(512)S(1)}, u32[]{:S(2)}, u32[]{:S(2)}) collective-permute-start(s32[512]{0:T(512)S(1)} %get-tuple-element.703), channel_id=1, source_target_pairs={{248,0},{0,8},{8,16},{16,24},{24,32},{32,40},{40,48},{48,56},{56,6... | collective-permute-start | bytes 6152 | tf_op jit(solution)/shard_map/while/body/eval_jaxpr/ppermute | solution.py:36
  256.0 14.3 %collective-permute-start = (bf16[512,256]{1,0:T(8,128)(2,1)S(1)}, bf16[512,256]{1,0:T(8,128)(2,1)S(1)}, u32[]{:S(2)}, u32[]{:S(2)}) collective-permute-start(bf16[512,256]{1,0:T(8,128)(2,1)S(1)} %get-tuple-element.702), channel_id=1, source_target_pairs={{248,0},{0,8},{8,16},{16,24},{24,32},{32,40},{40,48},{48,56},{56,6... | collective-permute-start | bytes 786440 | tf_op jit(solution)/shard_map/while/body/eval_jaxpr/ppermute | solution.py:36
  261.5 7.0 %collective-permute-start.1 = (s32[512]{0:T(512)S(1)}, s32[512]{0:T(512)S(1)}, u32[]{:S(2)}, u32[]{:S(2)}) collective-permute-start(s32[512]{0:T(512)S(1)} %get-tuple-element.703), channel_id=1, source_target_pairs={{248,0},{0,8},{8,16},{16,24},{24,32},{32,40},{40,48},{48,56},{56,6... | collective-permute-start | bytes 6152 | tf_op jit(solution)/shard_map/while/body/eval_jaxpr/ppermute | solution.py:36
Sparse Core Ops, SparseCore 0:
  9.2 37.7 all-gather.1
  277.6 101.4 reduce-scatter.1
where the time goes:
time: 387 us; the launch traced here: 386 us
  waiting for transfers between devices  187 us (48%)
  starting transfers between devices  99.6 us (26%)
  loops' own time  31 us (8%)
  matrix products  19.6 us (5%)
  local copies, waits for them, and re-layouts  18.7 us (5%)
  between operations  15.6 us (4%)
  other arithmetic  14.5 us (4%)
    reduce_scatter x1, waiting for transfers between devices, body(): lax.psum_scatter(partial_products.astype(jnp.bfloat16), ('head', 'grp'),...  102 us
    ppermute x32, starting transfers between devices, passed_along(): return lax.ppermute(block, axis, route)  99.5 us
    ppermute x32, waiting for transfers between devices, passed_along(): return lax.ppermute(block, axis, route)  54.7 us
    all_gather x1, waiting for transfers between devices, rows_first(): out, at, finished = (lax.all_gather(both, axis, axis=0, tiled=True), 0, [])  30.7 us
    another operation x1, loops' own time, body(): lax.fori_loop(1, reach + 1, advance, ((key_value, doc_ids), first_states))  30.4 us
    slice x16, local copies, waits for them, and re-layouts, step(): needed = (first_key <= query_set[4]) & (docs[width - 1] >= query_set[3])  9.34 us
  transfers between devices with their start and end apart: 34, of which 18 were waited for; matrix products, arithmetic and copies ran while one was open for 4% of the time, Pallas kernels for 0%

commit v1 on v0

--- a/solution.py
+++ b/solution.py
@@ -14,7 +14,13 @@
 def rows_first(arrays, axis, dims):
     turned = [jnp.moveaxis(a, dim, 0) for a, dim in zip(arrays, dims)]
     both = jnp.concatenate([t.reshape(len(t), -1) for t in turned], axis=1)
-    out, at, finished = (lax.all_gather(both, axis, axis=0, tiled=True), 0, [])
+    out, at, finished = (
+        jnp.concatenate(
+            lax.all_to_all(jnp.stack([both] * lax.axis_size(axis)), axis, 0, 0), axis=0
+        ),
+        0,
+        [],
+    )
     for t, dim in zip(turned, dims):
         section = out[:, at : at + t[0].size].reshape(-1, *t.shape[1:])
         finished.append(jnp.moveaxis(section, 0, dim))

time: 387 us -> 407 us (1.052)
  waiting for transfers between devices: 187 us -> 225 us
  starting transfers between devices: 99.6 us -> 82.8 us
  local copies, waits for them, and re-layouts: 18.7 us -> 26.3 us
    all_to_all x0 -> x1, waiting for transfers between devices: none -> 44.3 us  [rows_first(): lax.all_to_all(jnp.stack([both] * lax.axis_size(axis)), axis, 0, 0)]
    all_gather x1 -> x0, waiting for transfers between devices: 30.7 us -> none  [rows_first(): out, at, finished = (lax.all_gather(both, axis, axis=0, tiled=True), 0, [])]
    ppermute x32, waiting for transfers between devices: 54.7 us -> 78 us  [passed_along(): return lax.ppermute(block, axis, route)]
    ppermute x32, starting transfers between devices: 99.5 us -> 78.1 us  [passed_along(): return lax.ppermute(block, axis, route)]
    all_to_all x0 -> x1, starting transfers between devices: none -> 4.7 us  [rows_first(): lax.all_to_all(jnp.stack([both] * lax.axis_size(axis)), axis, 0, 0)]
  transfers between devices with their start and end apart: 34 -> 34, of which waited for: 18 -> 18; matrix products, arithmetic and copies ran while one was open for 4% -> 3% of each run, Pallas kernels for 0% -> 0%
where the time goes in v1:
time: 407 us; the launch traced here: 406 us
  waiting for transfers between devices  225 us (55%)
  starting transfers between devices  82.8 us (20%)
  loops' own time  29.2 us (7%)
  local copies, waits for them, and re-layouts  26.3 us (6%)
  matrix products  16 us (4%)
  between operations  15.6 us (4%)
  other arithmetic  10.7 us (3%)
    reduce_scatter x1, waiting for transfers between devices, body(): lax.psum_scatter(partial_products.astype(jnp.bfloat16), ('head', 'grp'),...  103 us
    ppermute x32, starting transfers between devices, passed_along(): return lax.ppermute(block, axis, route)  78.1 us
    ppermute x32, waiting for transfers between devices, passed_along(): return lax.ppermute(block, axis, route)  78 us
    all_to_all x1, waiting for transfers between devices, rows_first(): lax.all_to_all(jnp.stack([both] * lax.axis_size(axis)), axis, 0, 0)  44.3 us
    another operation x1, loops' own time, body(): lax.fori_loop(1, reach + 1, advance, ((key_value, doc_ids), first_states))  28.6 us
    slice x16, local copies, waits for them, and re-layouts, step(): needed = (first_key <= query_set[4]) & (docs[width - 1] >= query_set[3])  8.82 us
  transfers between devices with their start and end apart: 34, of which 18 were waited for; matrix products, arithmetic and copies ran while one was open for 3% of the time, Pallas kernels for 0%

profile of v1, /device:TPU:8, one launch (start us, length us, event | category | flops | bytes accessed | tf_op | source)
XLA Modules:
  0.0 405.8 jit_solution(15499870754857440148)
XLA Ops:
  8.3 2.3 stack.2
  10.6 4.7 %all-to-all-start = ((bf16[8,512,513]{1,2,0:T(8,128)(2,1)}), bf16[8,512,513]{1,2,0:T(8,128)(2,1)}, u32[]{:S(2)}, u32[]{:S(2)}) async-start(bf16[8,512,513]{1,2,0:T(8,128)(2,1)} %stack.2), calls=%async_computation | async-start | bytes 8519680 | tf_op jit(solution)/shard_map/all_to_all | solution.py:19
  19.6 1.8 multiply_cosine_fusion
  21.4 44.3 %all-to-all-done = bf16[8,512,513]{1,2,0:T(8,128)(2,1)} async-done(((bf16[8,512,513]{1,2,0:T(8,128)(2,1)}), bf16[8,512,513]{1,2,0:T(8,128)(2,1)}, u32[]{:S(2)}, u32[]{:S(2)}) %all-to-all-start) | async-done | bytes 4202528 | tf_op jit(solution)/shard_map/all_to_all | solution.py:19
  65.7 3.6 copy.17
  69.6 2.9 copy.15
  73.5 3.5 fusion.37
  81.6 1.8 subtract_convert_fusion
  83.7 5.6 %conditional.2 = ((f32[2048]{0:T(1024)S(1)}, f32[2048]{0:T(1024)S(1)}, f32[2048,128]{1,0:T(8,128)S(1)})) conditional(s32[]{:T(128)} %convert_element_type.61, (f32[2048]{0:T(1024)S(1)}, f32[2048]{0:T(1024)S(1)}, f32[2048,128]{1,0:T(8,128)S(1)}) %tuple.47, (s32[512]{0:T(512)S(1)}, s32[512]{0:T(512)S(1)}, s32[512]{0:T(512)S(1)}, s32[512]{0:T(512)S(1)}, ...), branch_computations={%region_1.2_spmd, %region_2.5_spmd} | conditional | flops 558370816 | bytes 16236576 | solution.py:114
  87.5 1.8 convolution_add_fusion
  89.3 199.5 %while.46 = (s32[]{:T(128)}, bf16[512,256]{1,0:T(8,128)(2,1)S(1)}, s32[512]{0:T(512)S(1)}, f32[2048]{0:T(1024)S(1)}, f32[2048]{0:T(1024)S(1)}, /*index=5*/f32[20...) while((s32[]{:T(128)}, bf16[512,256]{1,0:T(8,128)(2,1)S(1)}, ...), condition=%wide.region_10.11_spmd.clone, body=%wide.region_5.10_spmd.clone.sunk | while | flops 558371328 | bytes 17304096 | solution.py:179
  89.4 1.6 collective-permute-start
  92.8 4.8 %collective-permute-done.1 = s32[512]{0:T(512)S(1)} collective-permute-done((s32[512]{0:T(512)S(1)}, s32[512]{0:T(512)S(1)}, u32[]{:S(2)}, u32[]{:S(2)}) %collective-permute-start.1) | collective-permute-done | bytes 2080 | tf_op jit(solution)/shard_map/while/body/eval_jaxpr/ppermute | solution.py:42
  99.4 5.3 %conditional.5 = ((f32[2048]{0:T(1024)S(1)}, f32[2048]{0:T(1024)S(1)}, f32[2048,128]{1,0:T(8,128)S(1)})) conditional(s32[]{:T(128)} %convert_element_type.86, (f32[2048]{0:T(1024)S(1)}, f32[2048]{0:T(1024)S(1)}, f32[2048,128]{1,0:T(8,128)S(1)}) %tuple.76, (s32[]{:T(128)}, s32[512]{0:T(512)S(1)}, s32[512]{0:T(512)S(1)}, s32[512]{0:T(512)S(1)}, ...), branch_computations={%region_6.6_spmd, %region_7.9_spmd} | conditional | flops 558371328 | bytes 15716388 | solution.py:114
  101.2 1.6 fusion.20
  102.8 1.8 convolution_add_fusion.1
  107.8 4.2 %collective-permute-done.1 = s32[512]{0:T(512)S(1)} collective-permute-done((s32[512]{0:T(512)S(1)}, s32[512]{0:T(512)S(1)}, u32[]{:S(2)}, u32[]{:S(2)}) %collective-permute-start.1) | collective-permute-done | bytes 2080 | tf_op jit(solution)/shard_map/while/body/eval_jaxpr/ppermute | solution.py:42
  113.9 6.2 %collective-permute-start = (bf16[512,256]{1,0:T(8,128)(2,1)S(1)}, bf16[512,256]{1,0:T(8,128)(2,1)S(1)}, u32[]{:S(2)}, u32[]{:S(2)}) collective-permute-start(bf16[512,256]{1,0:T(8,128)(2,1)S(1)} %get-tuple-element.702), channel_id=1, source_target_pairs={{248,0},{0,8},{8,16},{16,24},{24,32},{32,40},{40,48},{48,56},{56,6... | collective-permute-start | bytes 786440 | tf_op jit(solution)/shard_map/while/body/eval_jaxpr/ppermute | solution.py:42
  120.7 4.2 %collective-permute-done.1 = s32[512]{0:T(512)S(1)} collective-permute-done((s32[512]{0:T(512)S(1)}, s32[512]{0:T(512)S(1)}, u32[]{:S(2)}, u32[]{:S(2)}) %collective-permute-start.1) | collective-permute-done | bytes 2080 | tf_op jit(solution)/shard_map/while/body/eval_jaxpr/ppermute | solution.py:42
  126.7 1.7 collective-permute-start
  129.1 7.2 %collective-permute-done.1 = s32[512]{0:T(512)S(1)} collective-permute-done((s32[512]{0:T(512)S(1)}, s32[512]{0:T(512)S(1)}, u32[]{:S(2)}, u32[]{:S(2)}) %collective-permute-start.1) | collective-permute-done | bytes 2080 | tf_op jit(solution)/shard_map/while/body/eval_jaxpr/ppermute | solution.py:42
  139.3 8.6 %collective-permute-done.1 = s32[512]{0:T(512)S(1)} collective-permute-done((s32[512]{0:T(512)S(1)}, s32[512]{0:T(512)S(1)}, u32[]{:S(2)}, u32[]{:S(2)}) %collective-permute-start.1) | collective-permute-done | bytes 2080 | tf_op jit(solution)/shard_map/while/body/eval_jaxpr/ppermute | solution.py:42
  151.2 8.2 %collective-permute-done.1 = s32[512]{0:T(512)S(1)} collective-permute-done((s32[512]{0:T(512)S(1)}, s32[512]{0:T(512)S(1)}, u32[]{:S(2)}, u32[]{:S(2)}) %collective-permute-start.1) | collective-permute-done | bytes 2080 | tf_op jit(solution)/shard_map/while/body/eval_jaxpr/ppermute | solution.py:42
  161.4 4.9 %collective-permute-start.1 = (s32[512]{0:T(512)S(1)}, s32[512]{0:T(512)S(1)}, u32[]{:S(2)}, u32[]{:S(2)}) collective-permute-start(s32[512]{0:T(512)S(1)} %get-tuple-element.703), channel_id=1, source_target_pairs={{248,0},{0,8},{8,16},{16,24},{24,32},{32,40},{40,48},{48,56},{56,6... | collective-permute-start | bytes 6152 | tf_op jit(solution)/shard_map/while/body/eval_jaxpr/ppermute | solution.py:42
  166.9 4.2 %collective-permute-done.1 = s32[512]{0:T(512)S(1)} collective-permute-done((s32[512]{0:T(512)S(1)}, s32[512]{0:T(512)S(1)}, u32[]{:S(2)}, u32[]{:S(2)}) %collective-permute-start.1) | collective-permute-done | bytes 2080 | tf_op jit(solution)/shard_map/while/body/eval_jaxpr/ppermute | solution.py:42
  174.2 2.6 collective-permute-start.1
  177.3 6.1 %collective-permute-done.1 = s32[512]{0:T(512)S(1)} collective-permute-done((s32[512]{0:T(512)S(1)}, s32[512]{0:T(512)S(1)}, u32[]{:S(2)}, u32[]{:S(2)}) %collective-permute-start.1) | collective-permute-done | bytes 2080 | tf_op jit(solution)/shard_map/while/body/eval_jaxpr/ppermute | solution.py:42
  185.2 4.6 %collective-permute-start = (bf16[512,256]{1,0:T(8,128)(2,1)S(1)}, bf16[512,256]{1,0:T(8,128)(2,1)S(1)}, u32[]{:S(2)}, u32[]{:S(2)}) collective-permute-start(bf16[512,256]{1,0:T(8,128)(2,1)S(1)} %get-tuple-element.702), channel_id=1, source_target_pairs={{248,0},{0,8},{8,16},{16,24},{24,32},{32,40},{40,48},{48,56},{56,6... | collective-permute-start | bytes 786440 | tf_op jit(solution)/shard_map/while/body/eval_jaxpr/ppermute | solution.py:42
  189.8 5.0 %collective-permute-start.1 = (s32[512]{0:T(512)S(1)}, s32[512]{0:T(512)S(1)}, u32[]{:S(2)}, u32[]{:S(2)}) collective-permute-start(s32[512]{0:T(512)S(1)} %get-tuple-element.703), channel_id=1, source_target_pairs={{248,0},{0,8},{8,16},{16,24},{24,32},{32,40},{40,48},{48,56},{56,6... | collective-permute-start | bytes 6152 | tf_op jit(solution)/shard_map/while/body/eval_jaxpr/ppermute | solution.py:42
  195.4 1.8 collective-permute-done.1
  199.0 4.1 %collective-permute-start = (bf16[512,256]{1,0:T(8,128)(2,1)S(1)}, bf16[512,256]{1,0:T(8,128)(2,1)S(1)}, u32[]{:S(2)}, u32[]{:S(2)}) collective-permute-start(bf16[512,256]{1,0:T(8,128)(2,1)S(1)} %get-tuple-element.702), channel_id=1, source_target_pairs={{248,0},{0,8},{8,16},{16,24},{24,32},{32,40},{40,48},{48,56},{56,6... | collective-permute-start | bytes 786440 | tf_op jit(solution)/shard_map/while/body/eval_jaxpr/ppermute | solution.py:42
  203.1 4.3 %collective-permute-start.1 = (s32[512]{0:T(512)S(1)}, s32[512]{0:T(512)S(1)}, u32[]{:S(2)}, u32[]{:S(2)}) collective-permute-start(s32[512]{0:T(512)S(1)} %get-tuple-element.703), channel_id=1, source_target_pairs={{248,0},{0,8},{8,16},{16,24},{24,32},{32,40},{40,48},{48,56},{56,6... | collective-permute-start | bytes 6152 | tf_op jit(solution)/shard_map/while/body/eval_jaxpr/ppermute | solution.py:42
  207.9 3.8 collective-permute-done.1
  213.6 1.6 collective-permute-start
  215.2 3.9 collective-permute-start.1
  219.6 5.3 %collective-permute-done.1 = s32[512]{0:T(512)S(1)} collective-permute-done((s32[512]{0:T(512)S(1)}, s32[512]{0:T(512)S(1)}, u32[]{:S(2)}, u32[]{:S(2)}) %collective-permute-start.1) | collective-permute-done | bytes 2080 | tf_op jit(solution)/shard_map/while/body/eval_jaxpr/ppermute | solution.py:42
  226.8 3.0 collective-permute-start.1
  230.4 6.8 %collective-permute-done.1 = s32[512]{0:T(512)S(1)} collective-permute-done((s32[512]{0:T(512)S(1)}, s32[512]{0:T(512)S(1)}, u32[]{:S(2)}, u32[]{:S(2)}) %collective-permute-start.1) | collective-permute-done | bytes 2080 | tf_op jit(solution)/shard_map/while/body/eval_jaxpr/ppermute | solution.py:42
  239.1 2.9 collective-permute-start.1
  242.6 6.1 %collective-permute-done.1 = s32[512]{0:T(512)S(1)} collective-permute-done((s32[512]{0:T(512)S(1)}, s32[512]{0:T(512)S(1)}, u32[]{:S(2)}, u32[]{:S(2)}) %collective-permute-start.1) | collective-permute-done | bytes 2080 | tf_op jit(solution)/shard_map/while/body/eval_jaxpr/ppermute | solution.py:42
  250.6 3.8 collective-permute-start.1
  255.0 5.2 %collective-permute-done.1 = s32[512]{0:T(512)S(1)} collective-permute-done((s32[512]{0:T(512)S(1)}, s32[512]{0:T(512)S(1)}, u32[]{:S(2)}, u32[]{:S(2)}) %collective-permute-start.1) | collective-permute-done | bytes 2080 | tf_op jit(solution)/shard_map/while/body/eval_jaxpr/ppermute | solution.py:42
  262.0 4.2 %collective-permute-start = (bf16[512,256]{1,0:T(8,128)(2,1)S(1)}, bf16[512,256]{1,0:T(8,128)(2,1)S(1)}, u32[]{:S(2)}, u32[]{:S(2)}) collective-permute-start(bf16[512,256]{1,0:T(8,128)(2,1)S(1)} %get-tuple-element.702), channel_id=1, source_target_pairs={{248,0},{0,8},{8,16},{16,24},{24,32},{32,40},{40,48},{48,56},{56,6... | collective-permute-start | bytes 786440 | tf_op jit(solution)/shard_map/while/body/eval_jaxpr/ppermute | solution.py:42
  266.2 4.8 %collective-permute-start.1 = (s32[512]{0:T(512)S(1)}, s32[512]{0:T(512)S(1)}, u32[]{:S(2)}, u32[]{:S(2)}) collective-permute-start(s32[512]{0:T(512)S(1)} %get-tuple-element.703), channel_id=1, source_target_pairs={{248,0},{0,8},{8,16},{16,24},{24,32},{32,40},{40,48},{48,56},{56,6... | collective-permute-start | bytes 6152 | tf_op jit(solution)/shard_map/while/body/eval_jaxpr/ppermute | solution.py:42
  274.2 5.0 %collective-permute-start = (bf16[512,256]{1,0:T(8,128)(2,1)S(1)}, bf16[512,256]{1,0:T(8,128)(2,1)S(1)}, u32[]{:S(2)}, u32[]{:S(2)}) collective-permute-start(bf16[512,256]{1,0:T(8,128)(2,1)S(1)} %get-tuple-element.702), channel_id=1, source_target_pairs={{248,0},{0,8},{8,16},{16,24},{24,32},{32,40},{40,48},{48,56},{56,6... | collective-permute-start | bytes 786440 | tf_op jit(solution)/shard_map/while/body/eval_jaxpr/ppermute | solution.py:42
  279.2 6.5 %collective-permute-start.1 = (s32[512]{0:T(512)S(1)}, s32[512]{0:T(512)S(1)}, u32[]{:S(2)}, u32[]{:S(2)}) collective-permute-start(s32[512]{0:T(512)S(1)} %get-tuple-element.703), channel_id=1, source_target_pairs={{248,0},{0,8},{8,16},{16,24},{24,32},{32,40},{40,48},{48,56},{56,6... | collective-permute-start | bytes 6152 | tf_op jit(solution)/shard_map/while/body/eval_jaxpr/ppermute | solution.py:42
  289.5 6.5 %convolution_convert_fusion = bf16[512,4096]{1,0:T(8,128)(2,1)} fusion(bf16[512,512]{1,0:T(8,128)(2,1)S(1)} %reshape.163, bf16[512,4096]{1,0:T(8,128)(2,1)} %param.14), kind=kOutput, calls=%fused_computation.48 | convolution fusion | flops 2149580800 | bytes 8912896 | tf_op jit(solution)/shard_map/dot_general | solution.py:181
  296.1 102.9 %reduce-scatter.2.cloned.1.call-done = bf16[512,512]{1,0:T(8,128)(2,1)} async-done(((bf16[512,4096]{1,0:T(8,128)(2,1)}), bf16[512,512]{1,0:T(8,128)(2,1)}) %reduce-scatter.2.cloned.1.call-update) | async-done | bytes 524304 | tf_op jit(solution)/shard_map/reduce_scatter | solution.py:182
  (180 shorter events, 34.5 us)
Async XLA Ops:
  10.6 6.5 %copy-start.1 = (s32[512]{0:T(512)S(1)}, s32[512]{0:T(512)}, u32[]{:S(2)}) copy-start(s32[512]{0:T(512)} %param.15) | copy-start | bytes 6148
  10.6 55.0 %all-to-all-start = ((bf16[8,512,513]{1,2,0:T(8,128)(2,1)}), bf16[8,512,513]{1,2,0:T(8,128)(2,1)}, u32[]{:S(2)}, u32[]{:S(2)}) async-start(bf16[8,512,513]{1,2,0:T(8,128)(2,1)} %stack.2), calls=%async_computation | async-start | bytes 8519680 | tf_op jit(solution)/shard_map/all_to_all | solution.py:19
  15.3 383.6 %reduce-scatter.2.cloned.1.call-start = ((), (), s32[]{:S(2)}) async-start(), calls=%async_computation.2 | async-start | bytes 4718592 | tf_op jit(solution)/shard_map/reduce_scatter | solution.py:182
  15.4 0.6 copy-start.3
  15.4 57.1 %copy-start.5 = (f32[512]{0:T(512)}, f32[512]{0:T(512)S(1)}, u32[]{:S(2)}) copy-start(f32[512]{0:T(512)S(1)} %get-tuple-element.592) | copy-start | bytes 6148
  19.6 49.7 %copy-start.6 = (f32[64]{0:T(128)}, f32[64]{0:T(128)S(1)}, u32[]{:S(2)}) copy-start(f32[64]{0:T(128)S(1)} %negate_power_fusion) | copy-start | bytes 772
  69.6 3.9 slice-start
  69.6 3.9 slice-start.1
  80.7 3.0 copy-start.2
  80.7 3.0 copy-start.4
  83.7 5.6 %copy-start = (bf16[512,256]{1,0:T(8,128)(2,1)S(1)}, bf16[512,256]{1,0:T(8,128)(2,1)}, u32[]{:S(2)}) copy-start(bf16[512,256]{1,0:T(8,128)(2,1)} %copy.12) | copy-start | bytes 786436
  83.7 5.6 %copy-start.7 = (s32[512]{0:T(512)S(1)}, s32[512]{0:T(512)}, u32[]{:S(2)}) copy-start(s32[512]{0:T(512)} %copy.32) | copy-start | bytes 6148
  89.4 10.0 %collective-permute-start = (bf16[512,256]{1,0:T(8,128)(2,1)S(1)}, bf16[512,256]{1,0:T(8,128)(2,1)S(1)}, u32[]{:S(2)}, u32[]{:S(2)}) collective-permute-start(bf16[512,256]{1,0:T(8,128)(2,1)S(1)} %get-tuple-element.702), channel_id=1, source_target_pairs={{248,0},{0,8},{8,16},{16,24},{24,32},{32,40},{40,48},{48,56},{56,6... | collective-permute-start | bytes 786440 | tf_op jit(solution)/shard_map/while/body/eval_jaxpr/ppermute | solution.py:42
  91.0 6.6 %collective-permute-start.1 = (s32[512]{0:T(512)S(1)}, s32[512]{0:T(512)S(1)}, u32[]{:S(2)}, u32[]{:S(2)}) collective-permute-start(s32[512]{0:T(512)S(1)} %get-tuple-element.703), channel_id=1, source_target_pairs={{248,0},{0,8},{8,16},{16,24},{24,32},{32,40},{40,48},{48,56},{56,6... | collective-permute-start | bytes 6152 | tf_op jit(solution)/shard_map/while/body/eval_jaxpr/ppermute | solution.py:42
  104.7 9.1 %collective-permute-start = (bf16[512,256]{1,0:T(8,128)(2,1)S(1)}, bf16[512,256]{1,0:T(8,128)(2,1)S(1)}, u32[]{:S(2)}, u32[]{:S(2)}) collective-permute-start(bf16[512,256]{1,0:T(8,128)(2,1)S(1)} %get-tuple-element.702), channel_id=1, source_target_pairs={{248,0},{0,8},{8,16},{16,24},{24,32},{32,40},{40,48},{48,56},{56,6... | collective-permute-start | bytes 786440 | tf_op jit(solution)/shard_map/while/body/eval_jaxpr/ppermute | solution.py:42
  106.0 6.1 %collective-permute-start.1 = (s32[512]{0:T(512)S(1)}, s32[512]{0:T(512)S(1)}, u32[]{:S(2)}, u32[]{:S(2)}) collective-permute-start(s32[512]{0:T(512)S(1)} %get-tuple-element.703), channel_id=1, source_target_pairs={{248,0},{0,8},{8,16},{16,24},{24,32},{32,40},{40,48},{48,56},{56,6... | collective-permute-start | bytes 6152 | tf_op jit(solution)/shard_map/while/body/eval_jaxpr/ppermute | solution.py:42
  113.9 12.7 %collective-permute-start = (bf16[512,256]{1,0:T(8,128)(2,1)S(1)}, bf16[512,256]{1,0:T(8,128)(2,1)S(1)}, u32[]{:S(2)}, u32[]{:S(2)}) collective-permute-start(bf16[512,256]{1,0:T(8,128)(2,1)S(1)} %get-tuple-element.702), channel_id=1, source_target_pairs={{248,0},{0,8},{8,16},{16,24},{24,32},{32,40},{40,48},{48,56},{56,6... | collective-permute-start | bytes 786440 | tf_op jit(solution)/shard_map/while/body/eval_jaxpr/ppermute | solution.py:42
  120.1 4.8 %collective-permute-start.1 = (s32[512]{0:T(512)S(1)}, s32[512]{0:T(512)S(1)}, u32[]{:S(2)}, u32[]{:S(2)}) collective-permute-start(s32[512]{0:T(512)S(1)} %get-tuple-element.703), channel_id=1, source_target_pairs={{248,0},{0,8},{8,16},{16,24},{24,32},{32,40},{40,48},{48,56},{56,6... | collective-permute-start | bytes 6152 | tf_op jit(solution)/shard_map/while/body/eval_jaxpr/ppermute | solution.py:42
  126.7 11.3 %collective-permute-start = (bf16[512,256]{1,0:T(8,128)(2,1)S(1)}, bf16[512,256]{1,0:T(8,128)(2,1)S(1)}, u32[]{:S(2)}, u32[]{:S(2)}) collective-permute-start(bf16[512,256]{1,0:T(8,128)(2,1)S(1)} %get-tuple-element.702), channel_id=1, source_target_pairs={{248,0},{0,8},{8,16},{16,24},{24,32},{32,40},{40,48},{48,56},{56,6... | collective-permute-start | bytes 786440 | tf_op jit(solution)/shard_map/while/body/eval_jaxpr/ppermute | solution.py:42
  128.4 7.9 %collective-permute-start.1 = (s32[512]{0:T(512)S(1)}, s32[512]{0:T(512)S(1)}, u32[]{:S(2)}, u32[]{:S(2)}) collective-permute-start(s32[512]{0:T(512)S(1)} %get-tuple-element.703), channel_id=1, source_target_pairs={{248,0},{0,8},{8,16},{16,24},{24,32},{32,40},{40,48},{48,56},{56,6... | collective-permute-start | bytes 6152 | tf_op jit(solution)/shard_map/while/body/eval_jaxpr/ppermute | solution.py:42
  138.1 11.5 %collective-permute-start = (bf16[512,256]{1,0:T(8,128)(2,1)S(1)}, bf16[512,256]{1,0:T(8,128)(2,1)S(1)}, u32[]{:S(2)}, u32[]{:S(2)}) collective-permute-start(bf16[512,256]{1,0:T(8,128)(2,1)S(1)} %get-tuple-element.702), channel_id=1, source_target_pairs={{248,0},{0,8},{8,16},{16,24},{24,32},{32,40},{40,48},{48,56},{56,6... | collective-permute-start | bytes 786440 | tf_op jit(solution)/shard_map/while/body/eval_jaxpr/ppermute | solution.py:42
  138.2 9.7 %collective-permute-start.1 = (s32[512]{0:T(512)S(1)}, s32[512]{0:T(512)S(1)}, u32[]{:S(2)}, u32[]{:S(2)}) collective-permute-start(s32[512]{0:T(512)S(1)} %get-tuple-element.703), channel_id=1, source_target_pairs={{248,0},{0,8},{8,16},{16,24},{24,32},{32,40},{40,48},{48,56},{56,6... | collective-permute-start | bytes 6152 | tf_op jit(solution)/shard_map/while/body/eval_jaxpr/ppermute | solution.py:42
  149.7 11.5 %collective-permute-start = (bf16[512,256]{1,0:T(8,128)(2,1)S(1)}, bf16[512,256]{1,0:T(8,128)(2,1)S(1)}, u32[]{:S(2)}, u32[]{:S(2)}) collective-permute-start(bf16[512,256]{1,0:T(8,128)(2,1)S(1)} %get-tuple-element.702), channel_id=1, source_target_pairs={{248,0},{0,8},{8,16},{16,24},{24,32},{32,40},{40,48},{48,56},{56,6... | collective-permute-start | bytes 786440 | tf_op jit(solution)/shard_map/while/body/eval_jaxpr/ppermute | solution.py:42
  149.8 9.7 %collective-permute-start.1 = (s32[512]{0:T(512)S(1)}, s32[512]{0:T(512)S(1)}, u32[]{:S(2)}, u32[]{:S(2)}) collective-permute-start(s32[512]{0:T(512)S(1)} %get-tuple-element.703), channel_id=1, source_target_pairs={{248,0},{0,8},{8,16},{16,24},{24,32},{32,40},{40,48},{48,56},{56,6... | collective-permute-start | bytes 6152 | tf_op jit(solution)/shard_map/while/body/eval_jaxpr/ppermute | solution.py:42
  161.3 11.5 %collective-permute-start = (bf16[512,256]{1,0:T(8,128)(2,1)S(1)}, bf16[512,256]{1,0:T(8,128)(2,1)S(1)}, u32[]{:S(2)}, u32[]{:S(2)}) collective-permute-start(bf16[512,256]{1,0:T(8,128)(2,1)S(1)} %get-tuple-element.702), channel_id=1, source_target_pairs={{248,0},{0,8},{8,16},{16,24},{24,32},{32,40},{40,48},{48,56},{56,6... | collective-permute-start | bytes 786440 | tf_op jit(solution)/shard_map/while/body/eval_jaxpr/ppermute | solution.py:42
  161.4 9.7 %collective-permute-start.1 = (s32[512]{0:T(512)S(1)}, s32[512]{0:T(512)S(1)}, u32[]{:S(2)}, u32[]{:S(2)}) collective-permute-start(s32[512]{0:T(512)S(1)} %get-tuple-element.703), channel_id=1, source_target_pairs={{248,0},{0,8},{8,16},{16,24},{24,32},{32,40},{40,48},{48,56},{56,6... | collective-permute-start | bytes 6152 | tf_op jit(solution)/shard_map/while/body/eval_jaxpr/ppermute | solution.py:42
  172.9 12.2 %collective-permute-start = (bf16[512,256]{1,0:T(8,128)(2,1)S(1)}, bf16[512,256]{1,0:T(8,128)(2,1)S(1)}, u32[]{:S(2)}, u32[]{:S(2)}) collective-permute-start(bf16[512,256]{1,0:T(8,128)(2,1)S(1)} %get-tuple-element.702), channel_id=1, source_target_pairs={{248,0},{0,8},{8,16},{16,24},{24,32},{32,40},{40,48},{48,56},{56,6... | collective-permute-start | bytes 786440 | tf_op jit(solution)/shard_map/while/body/eval_jaxpr/ppermute | solution.py:42
  174.2 9.3 %collective-permute-start.1 = (s32[512]{0:T(512)S(1)}, s32[512]{0:T(512)S(1)}, u32[]{:S(2)}, u32[]{:S(2)}) collective-permute-start(s32[512]{0:T(512)S(1)} %get-tuple-element.703), channel_id=1, source_target_pairs={{248,0},{0,8},{8,16},{16,24},{24,32},{32,40},{40,48},{48,56},{56,6... | collective-permute-start | bytes 6152 | tf_op jit(solution)/shard_map/while/body/eval_jaxpr/ppermute | solution.py:42
  185.2 13.6 %collective-permute-start = (bf16[512,256]{1,0:T(8,128)(2,1)S(1)}, bf16[512,256]{1,0:T(8,128)(2,1)S(1)}, u32[]{:S(2)}, u32[]{:S(2)}) collective-permute-start(bf16[512,256]{1,0:T(8,128)(2,1)S(1)} %get-tuple-element.702), channel_id=1, source_target_pairs={{248,0},{0,8},{8,16},{16,24},{24,32},{32,40},{40,48},{48,56},{56,6... | collective-permute-start | bytes 786440 | tf_op jit(solution)/shard_map/while/body/eval_jaxpr/ppermute | solution.py:42
  189.8 7.3 %collective-permute-start.1 = (s32[512]{0:T(512)S(1)}, s32[512]{0:T(512)S(1)}, u32[]{:S(2)}, u32[]{:S(2)}) collective-permute-start(s32[512]{0:T(512)S(1)} %get-tuple-element.703), channel_id=1, source_target_pairs={{248,0},{0,8},{8,16},{16,24},{24,32},{32,40},{40,48},{48,56},{56,6... | collective-permute-start | bytes 6152 | tf_op jit(solution)/shard_map/while/body/eval_jaxpr/ppermute | solution.py:42
  199.0 14.5 %collective-permute-start = (bf16[512,256]{1,0:T(8,128)(2,1)S(1)}, bf16[512,256]{1,0:T(8,128)(2,1)S(1)}, u32[]{:S(2)}, u32[]{:S(2)}) collective-permute-start(bf16[512,256]{1,0:T(8,128)(2,1)S(1)} %get-tuple-element.702), channel_id=1, source_target_pairs={{248,0},{0,8},{8,16},{16,24},{24,32},{32,40},{40,48},{48,56},{56,6... | collective-permute-start | bytes 786440 | tf_op jit(solution)/shard_map/while/body/eval_jaxpr/ppermute | solution.py:42
  203.1 8.7 %collective-permute-start.1 = (s32[512]{0:T(512)S(1)}, s32[512]{0:T(512)S(1)}, u32[]{:S(2)}, u32[]{:S(2)}) collective-permute-start(s32[512]{0:T(512)S(1)} %get-tuple-element.703), channel_id=1, source_target_pairs={{248,0},{0,8},{8,16},{16,24},{24,32},{32,40},{40,48},{48,56},{56,6... | collective-permute-start | bytes 6152 | tf_op jit(solution)/shard_map/while/body/eval_jaxpr/ppermute | solution.py:42
  213.6 13.1 %collective-permute-start = (bf16[512,256]{1,0:T(8,128)(2,1)S(1)}, bf16[512,256]{1,0:T(8,128)(2,1)S(1)}, u32[]{:S(2)}, u32[]{:S(2)}) collective-permute-start(bf16[512,256]{1,0:T(8,128)(2,1)S(1)} %get-tuple-element.702), channel_id=1, source_target_pairs={{248,0},{0,8},{8,16},{16,24},{24,32},{32,40},{40,48},{48,56},{56,6... | collective-permute-start | bytes 786440 | tf_op jit(solution)/shard_map/while/body/eval_jaxpr/ppermute | solution.py:42
  215.2 9.7 %collective-permute-start.1 = (s32[512]{0:T(512)S(1)}, s32[512]{0:T(512)S(1)}, u32[]{:S(2)}, u32[]{:S(2)}) collective-permute-start(s32[512]{0:T(512)S(1)} %get-tuple-element.703), channel_id=1, source_target_pairs={{248,0},{0,8},{8,16},{16,24},{24,32},{32,40},{40,48},{48,56},{56,6... | collective-permute-start | bytes 6152 | tf_op jit(solution)/shard_map/while/body/eval_jaxpr/ppermute | solution.py:42
  226.7 12.2 %collective-permute-start = (bf16[512,256]{1,0:T(8,128)(2,1)S(1)}, bf16[512,256]{1,0:T(8,128)(2,1)S(1)}, u32[]{:S(2)}, u32[]{:S(2)}) collective-permute-start(bf16[512,256]{1,0:T(8,128)(2,1)S(1)} %get-tuple-element.702), channel_id=1, source_target_pairs={{248,0},{0,8},{8,16},{16,24},{24,32},{32,40},{40,48},{48,56},{56,6... | collective-permute-start | bytes 786440 | tf_op jit(solution)/shard_map/while/body/eval_jaxpr/ppermute | solution.py:42
  226.8 10.4 %collective-permute-start.1 = (s32[512]{0:T(512)S(1)}, s32[512]{0:T(512)S(1)}, u32[]{:S(2)}, u32[]{:S(2)}) collective-permute-start(s32[512]{0:T(512)S(1)} %get-tuple-element.703), channel_id=1, source_target_pairs={{248,0},{0,8},{8,16},{16,24},{24,32},{32,40},{40,48},{48,56},{56,6... | collective-permute-start | bytes 6152 | tf_op jit(solution)/shard_map/while/body/eval_jaxpr/ppermute | solution.py:42
  239.0 11.4 %collective-permute-start = (bf16[512,256]{1,0:T(8,128)(2,1)S(1)}, bf16[512,256]{1,0:T(8,128)(2,1)S(1)}, u32[]{:S(2)}, u32[]{:S(2)}) collective-permute-start(bf16[512,256]{1,0:T(8,128)(2,1)S(1)} %get-tuple-element.702), channel_id=1, source_target_pairs={{248,0},{0,8},{8,16},{16,24},{24,32},{32,40},{40,48},{48,56},{56,6... | collective-permute-start | bytes 786440 | tf_op jit(solution)/shard_map/while/body/eval_jaxpr/ppermute | solution.py:42
  239.1 9.5 %collective-permute-start.1 = (s32[512]{0:T(512)S(1)}, s32[512]{0:T(512)S(1)}, u32[]{:S(2)}, u32[]{:S(2)}) collective-permute-start(s32[512]{0:T(512)S(1)} %get-tuple-element.703), channel_id=1, source_target_pairs={{248,0},{0,8},{8,16},{16,24},{24,32},{32,40},{40,48},{48,56},{56,6... | collective-permute-start | bytes 6152 | tf_op jit(solution)/shard_map/while/body/eval_jaxpr/ppermute | solution.py:42
  250.5 11.4 %collective-permute-start = (bf16[512,256]{1,0:T(8,128)(2,1)S(1)}, bf16[512,256]{1,0:T(8,128)(2,1)S(1)}, u32[]{:S(2)}, u32[]{:S(2)}) collective-permute-start(bf16[512,256]{1,0:T(8,128)(2,1)S(1)} %get-tuple-element.702), channel_id=1, source_target_pairs={{248,0},{0,8},{8,16},{16,24},{24,32},{32,40},{40,48},{48,56},{56,6... | collective-permute-start | bytes 786440 | tf_op jit(solution)/shard_map/while/body/eval_jaxpr/ppermute | solution.py:42
  250.6 9.6 %collective-permute-start.1 = (s32[512]{0:T(512)S(1)}, s32[512]{0:T(512)S(1)}, u32[]{:S(2)}, u32[]{:S(2)}) collective-permute-start(s32[512]{0:T(512)S(1)} %get-tuple-element.703), channel_id=1, source_target_pairs={{248,0},{0,8},{8,16},{16,24},{24,32},{32,40},{40,48},{48,56},{56,6... | collective-permute-start | bytes 6152 | tf_op jit(solution)/shard_map/while/body/eval_jaxpr/ppermute | solution.py:42
  262.0 12.1 %collective-permute-start = (bf16[512,256]{1,0:T(8,128)(2,1)S(1)}, bf16[512,256]{1,0:T(8,128)(2,1)S(1)}, u32[]{:S(2)}, u32[]{:S(2)}) collective-permute-start(bf16[512,256]{1,0:T(8,128)(2,1)S(1)} %get-tuple-element.702), channel_id=1, source_target_pairs={{248,0},{0,8},{8,16},{16,24},{24,32},{32,40},{40,48},{48,56},{56,6... | collective-permute-start | bytes 786440 | tf_op jit(solution)/shard_map/while/body/eval_jaxpr/ppermute | solution.py:42
  266.2 6.1 %collective-permute-start.1 = (s32[512]{0:T(512)S(1)}, s32[512]{0:T(512)S(1)}, u32[]{:S(2)}, u32[]{:S(2)}) collective-permute-start(s32[512]{0:T(512)S(1)} %get-tuple-element.703), channel_id=1, source_target_pairs={{248,0},{0,8},{8,16},{16,24},{24,32},{32,40},{40,48},{48,56},{56,6... | collective-permute-start | bytes 6152 | tf_op jit(solution)/shard_map/while/body/eval_jaxpr/ppermute | solution.py:42
  274.2 14.6 %collective-permute-start = (bf16[512,256]{1,0:T(8,128)(2,1)S(1)}, bf16[512,256]{1,0:T(8,128)(2,1)S(1)}, u32[]{:S(2)}, u32[]{:S(2)}) collective-permute-start(bf16[512,256]{1,0:T(8,128)(2,1)S(1)} %get-tuple-element.702), channel_id=1, source_target_pairs={{248,0},{0,8},{8,16},{16,24},{24,32},{32,40},{40,48},{48,56},{56,6... | collective-permute-start | bytes 786440 | tf_op jit(solution)/shard_map/while/body/eval_jaxpr/ppermute | solution.py:42
  279.2 7.8 %collective-permute-start.1 = (s32[512]{0:T(512)S(1)}, s32[512]{0:T(512)S(1)}, u32[]{:S(2)}, u32[]{:S(2)}) collective-permute-start(s32[512]{0:T(512)S(1)} %get-tuple-element.703), channel_id=1, source_target_pairs={{248,0},{0,8},{8,16},{16,24},{24,32},{32,40},{40,48},{48,56},{56,6... | collective-permute-start | bytes 6152 | tf_op jit(solution)/shard_map/while/body/eval_jaxpr/ppermute | solution.py:42
Sparse Core Ops, SparseCore 0:
  296.2 102.7 reduce-scatter.1
